TPU v7x, 32 devices: a whole 2x2x4 slice. The times are simulated.
32 devices in a mesh: groups: 2 (over y), seq: 16 (over z, x, core).
Axes of the slice: x: 2, y: 2, z: 4, core: 2. Of those that a mesh axis runs over, the one named last changes fastest.
Arguments:
- queries: bfloat16 [8192, 4096], P(('groups', 'seq')), parts along dimension 0, may hold values from -60 to 60
- vision: bfloat16 [512, 8192], P(('groups', 'seq')), parts along dimension 0, may hold values from -6 to 6
- w_key: bfloat16 [8192, 512], P('seq'), may hold values from -0.0625 to 0.0625
- w_value: bfloat16 [8192, 512], P('seq'), may hold values from -0.0625 to 0.0625
- key_gain: float32 [128], replicated, may hold values from 0.25 to 1.75
- image_range: int32 [8192, 2], P(('groups', 'seq')), parts along dimension 0, may hold values from 0 to 4, as said below
- image_counts: int32 [8], P('groups'), parts along dimension 0, may hold values from 32 to 64, as said below
Outputs:
- attended: bfloat16 [8192, 4096], P(('groups', 'seq')), parts along dimension 0
There are 2 independent parts, one for each index of `groups`. A program takes and returns all parts, laid end to end along the dimension named above; an argument that names none is the same for every part. Nothing has to cross between parts.
Inputs may be any that keep to these rules, and one draw needn't show every extreme that they name: A text token attends to the last 1 to 3 images placed at or before its position; tokens before the first image attend to none (both ends 0); image_range[t, 1] never falls along t. `image_counts`: the valid tokens of an image are the first slots of its 64 slots; some image fills all of them.
All inputs are finite; a program needn't handle non-finite values.
Results may differ from a plain program's by a relative error of at most 0.012.
The roundings to bfloat16 on the way count: a program that leaves them out, or rounds other values in their place, can miss the bound.
Values may be sent and summed in bfloat16 or wider, within the bound.
A program may use at most 64 MiB of HBM per device.

v0:
```python
import functools
import math

import jax
import jax.numpy as jnp
from jax import lax
from jax.experimental import pallas as pl
from jax.experimental.pallas import tpu as pltpu
from jax.sharding import PartitionSpec as P

MESH = pl.DeviceIdType.MESH
CORES = 2
CHUNKS = 1
STEPS = 2
DIRECT = (1,)
VALUE_LINK = jnp.bfloat16


def normed_keys(raw_keys, gain):
    head_size = gain.shape[1]
    heads = []
    for start in range(0, raw_keys.shape[1], head_size):
        head = raw_keys[:, start : start + head_size]
        inverse_rms = lax.rsqrt(jnp.mean(head * head, axis=1, keepdims=True) + 1e-05)
        heads.append((head * inverse_rms * gain).astype(jnp.bfloat16))
    return jnp.concatenate(heads, axis=1)


def project_kernel(
    chips, vision_hbm, w_key_hbm, w_value_hbm, gain_ref, keys_hbm, values_hbm,
    vision, columns, w_both, partial, key_sent, key_arrived, value_sent, value_arrived, rows_out,
    load_sem, weight_load_sem, weight_send_sem, weight_recv_sem,
    vision_send, vision_recv, partial_send, partial_recv,
    gather_send, gather_recv, pair_send, pair_recv, forward_send, forward_recv, out_sem,
):
    me = lax.axis_index("seq")
    group = lax.axis_index("groups")
    chip, core = me // CORES, me % CORES
    half, place, parity = chips // 2, chip // 2, chip % 2
    depth = w_key_hbm.shape[0]
    width = CORES * depth
    rows = columns.shape[2]
    partner = (group, chip * CORES + (1 - core))
    pair = (group, (place * 2 + 1 - parity) * CORES + core)
    peers = [lax.rem(chip + step, chips) for step in range(1, chips)]
    line = [lax.rem(place + step, half) * 2 + parity for step in range(1, half)]

    def at(chip_index):
        return (group, chip_index * CORES + core)

    load = pltpu.make_async_copy(vision_hbm, vision, load_sem)
    load.start()
    mine = pl.ds(pl.multiple_of(core * depth, depth), depth)
    weights = [w_key_hbm, w_value_hbm]
    weight_loads = [
        pltpu.make_async_copy(weights[i], w_both.at[i, mine], weight_load_sem.at[i]) for i in range(2)
    ]
    for copy in weight_loads:
        copy.start()

    barrier = pltpu.get_barrier_semaphore()
    for peer in peers:
        pl.semaphore_signal(barrier, inc=1, device_id=at(peer), device_id_type=MESH)
    pl.semaphore_signal(barrier, inc=1, device_id=partner, device_id_type=MESH)
    pl.semaphore_wait(barrier, chips)

    def remote(src, dst, send_sem, recv_sem, device):
        return pltpu.make_async_remote_copy(
            src_ref=src, dst_ref=dst, send_sem=send_sem, recv_sem=recv_sem,
            device_id=device, device_id_type=MESH,
        )

    load.wait()
    vision_copies = []
    for chunk in range(CHUNKS):
        own_rows = pl.ds(chunk * rows, rows)
        chunk_copies = []
        for step, peer in enumerate(peers):
            part = pl.ds(pl.multiple_of(peer * width, 128), width)
            copy = remote(
                vision.at[own_rows, part], columns.at[chunk, chip],
                vision_send.at[chunk, step], vision_recv.at[chunk, step], at(peer),
            )
            copy.start()
            chunk_copies.append(copy)
        vision_copies.append(chunk_copies)
    weight_sends = [
        remote(weights[i], w_both.at[i, mine], weight_send_sem.at[i], weight_recv_sem.at[i], partner)
        for i in range(2)
    ]
    for copy in weight_sends:
        copy.start()
    for chunk in range(CHUNKS):
        columns[chunk, chip] = vision[chunk * rows : (chunk + 1) * rows, pl.ds(pl.multiple_of(chip * width, 128), width)]
    for copy in weight_loads:
        copy.wait()
    for copy in weight_sends:
        copy.wait()

    streams = [(chunk, i) for chunk in range(CHUNKS) for i in range(2)]
    partial_copies = []
    for stream, (chunk, i) in enumerate(streams):
        if i == 0:
            for copy in vision_copies[chunk]:
                copy.wait()
        left = columns[chunk].reshape(chips * rows, width)
        product = jnp.dot(left, w_both[i], preferred_element_type=jnp.float32).reshape(chips, rows, -1)
        if i == 0:
            sent, landed = key_sent, key_arrived
            sent[chunk] = product
        else:
            sent, landed = value_sent, value_arrived
            sent[chunk] = product.astype(sent.dtype)
            partial[...] = product
        stream_copies = []
        for step, peer in enumerate(peers):
            copy = remote(
                sent.at[chunk, peer], landed.at[chunk, step],
                partial_send.at[stream, step], partial_recv.at[stream, step], at(peer),
            )
            copy.start()
            stream_copies.append(copy)
        if i == 0:
            own = None
        else:
            own = partial[chip]
        partial_copies.append((stream_copies, own))

    def block(stream, source):
        chunk, i = streams[stream]
        return rows_out.at[i, source, pl.ds(chunk * rows, rows)]

    def move(stream, source, send_sem, recv_sem, slot, device):
        ref = block(stream, source)
        copy = remote(ref, ref, send_sem.at[stream, slot], recv_sem.at[stream, slot], device)
        copy.start()
        return copy

    gathers, pairs, forwards = {}, {}, ([], [])

    def finish(stream):
        chunk, i = streams[stream]
        copies, total = partial_copies[stream]
        if i == 0:
            total = key_sent[chunk, chip]
        landed = key_arrived if i == 0 else value_arrived
        for step, copy in enumerate(copies):
            copy.wait()
            total = total + landed[chunk, step].astype(jnp.float32)
        done = normed_keys(total, gain_ref[...]) if i == 0 else total.astype(jnp.bfloat16)
        rows_out[i, me, chunk * rows : (chunk + 1) * rows] = done
        targets = peers if i in DIRECT else line
        gathers[stream] = [
            move(stream, me, gather_send, gather_recv, step, at(peer)) for step, peer in enumerate(targets)
        ]
        pairs[stream] = [] if i in DIRECT else [move(stream, me, pair_send, pair_recv, 0, pair)]
        forwards[streams[stream][1]].append(move(stream, me, forward_send, forward_recv, 0, partner))

    def pass_line(stream):
        chunk, i = streams[stream]
        for step, copy in enumerate(gathers[stream]):
            copy.wait()
            if i in DIRECT:
                source = lax.rem(chip + chips - 1 - step, chips) * CORES + core
            else:
                source = (lax.rem(place + half - 1 - step, half) * 2 + parity) * CORES + core
                pairs[stream].append(move(stream, source, pair_send, pair_recv, step + 1, pair))
            forwards[streams[stream][1]].append(move(stream, source, forward_send, forward_recv, step + 1, partner))

    def pass_pair(stream):
        for step, copy in enumerate(pairs[stream]):
            copy.wait()
            source = (lax.rem(place + half - step, half) * 2 + 1 - parity) * CORES + core
            forwards[streams[stream][1]].append(move(stream, source, forward_send, forward_recv, half + step, partner))

    count = len(streams)
    for turn in range(count + 2):
        for lag, act in enumerate((finish, pass_line, pass_pair)):
            if 0 <= turn - lag < count:
                act(turn - lag)
    outs = [
        pltpu.make_async_copy(rows_out.at[i], out, out_sem.at[i]) for i, out in enumerate([keys_hbm, values_hbm])
    ]
    for i in range(2):
        for copy in forwards[i]:
            copy.wait()
        outs[i].start()
    for copy in outs:
        copy.wait()


def project(vision, w_key, w_value, key_gain):
    shards = lax.axis_size("seq")
    chips = shards // CORES
    rows, full = vision.shape
    piece = rows // CHUNKS
    depth, kv_width = w_key.shape
    gathered = jax.ShapeDtypeStruct((shards, rows, kv_width), jnp.bfloat16)
    dma = pltpu.SemaphoreType.DMA
    hops, half, streams = chips - 1, chips // 2, 2 * CHUNKS
    f32, bf16 = jnp.float32, jnp.bfloat16
    keys, values = pl.pallas_call(
        functools.partial(project_kernel, chips),
        out_shape=(gathered, gathered),
        in_specs=[pl.BlockSpec(memory_space=pl.ANY)] * 3 + [pl.BlockSpec(memory_space=pltpu.VMEM)],
        out_specs=(pl.BlockSpec(memory_space=pl.ANY),) * 2,
        scratch_shapes=[
            pltpu.VMEM((rows, full), bf16),
            pltpu.VMEM((CHUNKS, chips, piece, CORES * depth), bf16),
            pltpu.VMEM((2, CORES * depth, kv_width), bf16),
            pltpu.VMEM((chips, piece, kv_width), f32),
            pltpu.VMEM((CHUNKS, chips, piece, kv_width), f32),
            pltpu.VMEM((CHUNKS, hops, piece, kv_width), f32),
            pltpu.VMEM((CHUNKS, chips, piece, kv_width), VALUE_LINK),
            pltpu.VMEM((CHUNKS, hops, piece, kv_width), VALUE_LINK),
            pltpu.VMEM((2, shards, rows, kv_width), bf16),
            dma, dma((2,)), dma((2,)), dma((2,)),
            dma((CHUNKS, hops)), dma((CHUNKS, hops)), dma((streams, hops)), dma((streams, hops)),
            dma((streams, hops)), dma((streams, hops)),
            dma((streams, half)), dma((streams, half)),
            dma((streams, chips)), dma((streams, chips)), dma((2,)),
        ],
        compiler_params=pltpu.CompilerParams(collective_id=0, has_side_effects=True),
        name="project",
    )(vision, w_key, w_value, key_gain.reshape(1, -1))
    return keys.reshape(shards * rows, kv_width), values.reshape(shards * rows, kv_width)


def attend_kernel(slot_count, head_size, counts_ref, range_ref, queries_ref, keys_ref, values_ref, out_ref, bias):
    vision_rows = keys_ref.shape[0]

    @pl.when(pl.program_id(0) == 0)
    def _():
        low_ends, high_ends = range_ref[0:1, :], range_ref[1:2, :]
        index = lax.broadcasted_iota(jnp.int32, (vision_rows, 1), 0)
        image = jnp.zeros_like(index)
        first = jnp.zeros_like(index)
        limit = jnp.zeros_like(index) + counts_ref[0]
        for i in range(1, counts_ref.shape[0]):
            past = index >= i * slot_count
            image = jnp.where(past, i, image)
            first = jnp.where(past, i * slot_count, first)
            limit = jnp.where(past, counts_ref[i], limit)
        live_image = jnp.where(index - first < limit, image, -1)
        allowed = (live_image >= low_ends) & (live_image < high_ends)
        bias[...] = jnp.where(allowed, 0.0, -1e30).T

    scale = math.log2(math.e) / math.sqrt(head_size)
    kv_block = keys_ref.shape[1] // head_size
    group_width = queries_ref.shape[1] // kv_block
    ones = jnp.ones((vision_rows, head_size), jnp.bfloat16)
    for kv_head in range(kv_block):
        kv_part = pl.ds(kv_head * head_size, head_size)
        keys = keys_ref[:, kv_part]
        values = jnp.concatenate([values_ref[:, kv_part], ones], axis=1)
        for start in range(kv_head * group_width, (kv_head + 1) * group_width, head_size):
            head = pl.ds(start, head_size)
            scores = lax.dot_general(
                queries_ref[:, head], keys, (((1,), (1,)), ((), ())), preferred_element_type=jnp.float32
            )
            scores = scores + bias[...]
            row_max = jnp.maximum(jnp.max(scores, axis=1, keepdims=True), -1e29)
            weights = jnp.exp2((scores - row_max) * scale).astype(jnp.bfloat16)
            summed = jnp.dot(weights, values, preferred_element_type=jnp.float32)
            weighted, row_sum = summed[:, :head_size], summed[:, head_size:]
            out_ref[:, head] = (weighted / jnp.where(row_sum > 0.0, row_sum, 1.0)).astype(jnp.bfloat16)


def attend(queries, keys, values, image_range, image_counts, head_size):
    tokens, query_width = queries.shape
    vision_rows, kv_width = keys.shape
    kv_heads = kv_width // head_size
    steps = math.gcd(kv_heads, STEPS)
    group_width = query_width // steps
    kv_block = kv_width // steps
    slot_count = vision_rows // image_counts.shape[0]
    return pl.pallas_call(
        functools.partial(attend_kernel, slot_count, head_size),
        out_shape=jax.ShapeDtypeStruct(queries.shape, jnp.bfloat16),
        grid=(steps,),
        in_specs=[
            pl.BlockSpec(memory_space=pltpu.SMEM),
            pl.BlockSpec((2, tokens), lambda h: (0, 0)),
            pl.BlockSpec((tokens, group_width), lambda h: (0, h)),
            pl.BlockSpec((vision_rows, kv_block), lambda h: (0, h)),
            pl.BlockSpec((vision_rows, kv_block), lambda h: (0, h)),
        ],
        out_specs=pl.BlockSpec((tokens, group_width), lambda h: (0, h)),
        scratch_shapes=[pltpu.VMEM((tokens, vision_rows), jnp.float32)],
        name="attend",
    )(image_counts, image_range.T, queries, keys, values)


def per_device(queries, vision, w_key, w_value, key_gain, image_range, image_counts):
    keys, values = project(vision, w_key, w_value, key_gain)
    return attend(queries, keys, values, image_range, image_counts, key_gain.shape[0])


def solution(mesh):
    placed = (
        P(("groups", "seq"), None),
        P(("groups", "seq"), None),
        P("seq", None),
        P("seq", None),
        P(),
        P(("groups", "seq"), None),
        P("groups"),
    )
    return jax.shard_map(
        per_device,
        mesh=mesh,
        in_specs=placed,
        out_specs=P(("groups", "seq"), None),
        check_vma=False,
    )
```

profile of v0, /device:TPU:0, one launch (start us, length us, event | category | flops | bytes accessed | tf_op | source)
XLA Modules:
  0.0 38.9 jit_solution(15783497312908679465)
XLA Ops:
  0.0 33.4 %project.1 = (bf16[16,16,512]{2,1,0:T(8,128)(2,1)}, bf16[16,16,512]{2,1,0:T(8,128)(2,1)}) custom-call(bf16[16,8192]{1,0:T(8,128)(2,1)} %vision_hbm.1, bf16[512,512]{1,0:T(8,128)(2,1)} %w_key_hbm.1, bf16[512,512]{1,0:T(8,128)(2,1)} %w_value_hbm.1, f32[1,128]{1,0:T(1,128)} %bitcast.7), custom_call_target="tpu_custom_call" | custom-call | tf_op jit(solution)/shard_map/project/pallas_call | solution.py:202
  33.4 5.5 %attend.1 = bf16[256,4096]{1,0:T(8,128)(2,1)} custom-call(s32[4]{0:T(128)} %counts_ref.1, s32[2,256]{1,0:T(2,128)} %bitcast.6, bf16[256,4096]{1,0:T(8,128)(2,1)} %queries_ref.1, bf16[256,512]{1,0:T(8,128)(2,1)} %bitcast.4, bf16[256,512]{1,0:T(8,128)(2,1)} %bitcast.5), custom_call_target="tpu_custom_call" | custom-call | tf_op jit(solution)/shard_map/attend/pallas_call | solution.py:277
where the time goes:
time: 39 us; the launch traced here: 38.9 us
  Pallas kernels  38.9 us (100%)
    pallas_call x1, Pallas kernels, project(): pl.pallas_call(functools.partial(project_kernel, chips), out_shape=(gathe...  33.4 us
    pallas_call x1, Pallas kernels, attend(): pl.pallas_call(functools.partial(attend_kernel, slot_count, head_size), o...  5.47 us

commit v1 on v0

--- a/solution.py
+++ b/solution.py
@@ -13,7 +13,7 @@
 CHUNKS = 1
 STEPS = 2
 DIRECT = (1,)
-VALUE_LINK = jnp.bfloat16
+LINK = jnp.bfloat16
 
 
 def normed_keys(raw_keys, gain):
@@ -28,7 +28,7 @@
 
 def project_kernel(
     chips, vision_hbm, w_key_hbm, w_value_hbm, gain_ref, keys_hbm, values_hbm,
-    vision, columns, w_both, partial, key_sent, key_arrived, value_sent, value_arrived, rows_out,
+    vision, columns, w_both, partial, partial_k, key_sent, key_arrived, value_sent, value_arrived, rows_out,
     load_sem, weight_load_sem, weight_send_sem, weight_recv_sem,
     vision_send, vision_recv, partial_send, partial_recv,
     gather_send, gather_recv, pair_send, pair_recv, forward_send, forward_recv, out_sem,
@@ -107,7 +107,8 @@
         product = jnp.dot(left, w_both[i], preferred_element_type=jnp.float32).reshape(chips, rows, -1)
         if i == 0:
             sent, landed = key_sent, key_arrived
-            sent[chunk] = product
+            sent[chunk] = product.astype(sent.dtype)
+            partial_k[...] = product
         else:
             sent, landed = value_sent, value_arrived
             sent[chunk] = product.astype(sent.dtype)
@@ -142,7 +143,7 @@
         chunk, i = streams[stream]
         copies, total = partial_copies[stream]
         if i == 0:
-            total = key_sent[chunk, chip]
+            total = partial_k[chip]
         landed = key_arrived if i == 0 else value_arrived
         for step, copy in enumerate(copies):
             copy.wait()
@@ -209,10 +210,11 @@
             pltpu.VMEM((CHUNKS, chips, piece, CORES * depth), bf16),
             pltpu.VMEM((2, CORES * depth, kv_width), bf16),
             pltpu.VMEM((chips, piece, kv_width), f32),
-            pltpu.VMEM((CHUNKS, chips, piece, kv_width), f32),
-            pltpu.VMEM((CHUNKS, hops, piece, kv_width), f32),
-            pltpu.VMEM((CHUNKS, chips, piece, kv_width), VALUE_LINK),
-            pltpu.VMEM((CHUNKS, hops, piece, kv_width), VALUE_LINK),
+            pltpu.VMEM((chips, piece, kv_width), f32),
+            pltpu.VMEM((CHUNKS, chips, piece, kv_width), LINK),
+            pltpu.VMEM((CHUNKS, hops, piece, kv_width), LINK),
+            pltpu.VMEM((CHUNKS, chips, piece, kv_width), LINK),
+            pltpu.VMEM((CHUNKS, hops, piece, kv_width), LINK),
             pltpu.VMEM((2, shards, rows, kv_width), bf16),
             dma, dma((2,)), dma((2,)), dma((2,)),
             dma((CHUNKS, hops)), dma((CHUNKS, hops)), dma((streams, hops)), dma((streams, hops)),

time: 39 us -> 35.9 us (0.921)
  Pallas kernels: 38.9 us -> 35.7 us
    pallas_call x1, Pallas kernels: 33.4 us -> 30.3 us  [project(): pl.pallas_call(functools.partial(project_kernel, chips), out_shape=(gathe...]
where the time goes in v1:
time: 35.9 us; the launch traced here: 35.7 us
  Pallas kernels  35.7 us (99%)
    pallas_call x1, Pallas kernels, project(): pl.pallas_call(functools.partial(project_kernel, chips), out_shape=(gathe...  30.3 us
    pallas_call x1, Pallas kernels, attend(): pl.pallas_call(functools.partial(attend_kernel, slot_count, head_size), o...  5.47 us

profile of v1, /device:TPU:0, one launch (start us, length us, event | category | flops | bytes accessed | tf_op | source)
XLA Modules:
  0.0 35.7 jit_solution(17672983110253309501)
XLA Ops:
  0.0 30.3 %project.1 = (bf16[16,16,512]{2,1,0:T(8,128)(2,1)}, bf16[16,16,512]{2,1,0:T(8,128)(2,1)}) custom-call(bf16[16,8192]{1,0:T(8,128)(2,1)} %vision_hbm.1, bf16[512,512]{1,0:T(8,128)(2,1)} %w_key_hbm.1, bf16[512,512]{1,0:T(8,128)(2,1)} %w_value_hbm.1, f32[1,128]{1,0:T(1,128)} %bitcast.7), custom_call_target="tpu_custom_call" | custom-call | tf_op jit(solution)/shard_map/project/pallas_call | solution.py:203
  30.3 5.5 %attend.1 = bf16[256,4096]{1,0:T(8,128)(2,1)} custom-call(s32[4]{0:T(128)} %counts_ref.1, s32[2,256]{1,0:T(2,128)} %bitcast.6, bf16[256,4096]{1,0:T(8,128)(2,1)} %queries_ref.1, bf16[256,512]{1,0:T(8,128)(2,1)} %bitcast.4, bf16[256,512]{1,0:T(8,128)(2,1)} %bitcast.5), custom_call_target="tpu_custom_call" | custom-call | tf_op jit(solution)/shard_map/attend/pallas_call | solution.py:279

commit v2 on v1

v2 whole, which is shorter than its diff:
```python
import functools
import math

import jax
import jax.numpy as jnp
from jax import lax
from jax.experimental import pallas as pl
from jax.experimental.pallas import tpu as pltpu
from jax.sharding import PartitionSpec as P

MESH = pl.DeviceIdType.MESH
CORES = 2
STEPS = 2
STORE_HEADS = 4
EARLY_HEADS = 24
LINK = jnp.bfloat16
MASKED = -1e30
MIB = 1024 * 1024
WEIGHTS_MAX = 8 * MIB


def normed_keys(raw_keys, gain):
    head_size = gain.shape[1]
    heads = []
    for start in range(0, raw_keys.shape[1], head_size):
        head = raw_keys[:, start : start + head_size]
        inverse_rms = lax.rsqrt(jnp.mean(head * head, axis=1, keepdims=True) + 1e-05)
        heads.append((head * inverse_rms * gain).astype(jnp.bfloat16))
    return jnp.concatenate(heads, axis=1)


def token_marks(range_ref, images, width):
    low_ends, high_ends = range_ref[0:1, :], range_ref[1:2, :]
    image = lax.broadcasted_iota(jnp.int32, (width, 1), 0)
    outside = (image < low_ends) | (image >= high_ends)
    marked = ((image < images) & outside) | (image == images)
    return jnp.where(marked, 1.0, 0.0).T.astype(jnp.bfloat16)


def row_marks(counts_ref, vision_rows, width):
    images = counts_ref.shape[0]
    slot_count = vision_rows // images
    index = lax.broadcasted_iota(jnp.int32, (vision_rows, width), 0)
    column = lax.broadcasted_iota(jnp.int32, (vision_rows, width), 1)
    image = jnp.zeros_like(index)
    first = jnp.zeros_like(index)
    limit = jnp.zeros_like(index) + counts_ref[0]
    for i in range(1, images):
        past = index >= i * slot_count
        image = jnp.where(past, i, image)
        first = jnp.where(past, i * slot_count, first)
        limit = jnp.where(past, counts_ref[i], limit)
    dead = index - first >= limit
    return jnp.where((column == image) | ((column == images) & dead), MASKED, 0.0).astype(jnp.bfloat16)


def project_kernel(chips, fused, *refs):
    if fused:
        vision_hbm, w_key_hbm, w_value_hbm, gain_hbm, counts_hbm, range_hbm, queries_hbm = refs[:7]
        weights_ref, values_ref = refs[7:9]
        counts_ref, range_ref, queries, marks, row_mark, extra_sem = refs[9:15]
        refs = refs[15:]
    else:
        vision_hbm, w_key_hbm, w_value_hbm, gain_hbm, keys_ref, values_ref = refs[:6]
        refs = refs[6:]
    (
        gain_ref, gain_sem, vision, columns, w_both, partial, sent, arrived, gathered,
        load_sem, weight_load_sem, weight_send_sem, weight_recv_sem, vision_send, vision_recv,
        partial_send, partial_recv, gather_send, gather_recv, forward_send, forward_recv,
    ) = refs
    me = lax.axis_index("seq")
    group = lax.axis_index("groups")
    chip, core = me // CORES, me % CORES
    depth = w_key_hbm.shape[0]
    width = CORES * depth
    rows = columns.shape[1]
    partner = (group, chip * CORES + (1 - core))
    peers = [lax.rem(chip + step, chips) for step in range(1, chips)]

    def at(chip_index):
        return (group, chip_index * CORES + core)

    load = pltpu.make_async_copy(vision_hbm, vision, load_sem)
    load.start()
    mine = pl.ds(pl.multiple_of(core * depth, depth), depth)
    weights = [w_key_hbm, w_value_hbm]
    weight_loads = [
        pltpu.make_async_copy(weights[i], w_both.at[i, mine], weight_load_sem.at[i]) for i in range(2)
    ]
    for copy in weight_loads:
        copy.start()
    gain_load = pltpu.make_async_copy(gain_hbm, gain_ref, gain_sem)
    gain_load.start()
    if fused:
        counts_load, range_load, query_load = [
            pltpu.make_async_copy(source, target, extra_sem.at[i])
            for i, (source, target) in enumerate(
                [(counts_hbm, counts_ref), (range_hbm, range_ref), (queries_hbm, queries)]
            )
        ]
        counts_load.start()
        range_load.start()
        query_load.start()

    barrier = pltpu.get_barrier_semaphore()
    for peer in peers:
        pl.semaphore_signal(barrier, inc=1, device_id=at(peer), device_id_type=MESH)
    pl.semaphore_signal(barrier, inc=1, device_id=partner, device_id_type=MESH)
    pl.semaphore_wait(barrier, chips)

    def remote(src, dst, send_sem, recv_sem, device):
        return pltpu.make_async_remote_copy(
            src_ref=src, dst_ref=dst, send_sem=send_sem, recv_sem=recv_sem,
            device_id=device, device_id_type=MESH,
        )

    load.wait()
    vision_copies = []
    for step, peer in enumerate(peers):
        part = pl.ds(pl.multiple_of(peer * width, 128), width)
        copy = remote(vision.at[:, part], columns.at[chip], vision_send.at[step], vision_recv.at[step], at(peer))
        copy.start()
        vision_copies.append(copy)
    for copy in weight_loads:
        copy.wait()
    weight_sends = [
        remote(w_both.at[i, mine], w_both.at[i, mine], weight_send_sem.at[i], weight_recv_sem.at[i], partner)
        for i in range(2)
    ]
    for copy in weight_sends:
        copy.start()
    columns[chip] = vision[:, pl.ds(pl.multiple_of(chip * width, 128), width)]
    gain_load.wait()
    if fused:
        counts_load.wait()
        range_load.wait()
        marks[...] = token_marks(range_ref, counts_ref.shape[0], marks.shape[1])
        row_mark[...] = row_marks(counts_ref, *row_mark.shape)
    for copy in weight_sends:
        copy.wait()
    for copy in vision_copies:
        copy.wait()

    partial_copies = []
    for i in range(2):
        left = columns[...].reshape(chips * rows, width)
        product = jnp.dot(left, w_both[i], preferred_element_type=jnp.float32).reshape(chips, rows, -1)
        sent[i] = product.astype(sent.dtype)
        partial[...] = product
        stream_copies = []
        for step, peer in enumerate(peers):
            copy = remote(
                sent.at[i, peer], arrived.at[i, step], partial_send.at[i, step], partial_recv.at[i, step], at(peer),
            )
            copy.start()
            stream_copies.append(copy)
        partial_copies.append((stream_copies, partial[chip]))

    def forward(i, source, slot):
        ref = gathered.at[i, source]
        copy = remote(ref, ref, forward_send.at[i, slot], forward_recv.at[i, slot], partner)
        copy.start()
        return copy

    gathers, forwards = [], ([], [])
    for i in range(2):
        copies, total = partial_copies[i]
        for step, copy in enumerate(copies):
            copy.wait()
            total = total + arrived[i, step].astype(jnp.float32)
        done = normed_keys(total, gain_ref[...]) if i == 0 else total.astype(jnp.bfloat16)
        gathered[i, me] = done
        ref = gathered.at[i, me]
        stream_copies = []
        for step, peer in enumerate(peers):
            copy = remote(ref, ref, gather_send.at[i, step], gather_recv.at[i, step], at(peer))
            copy.start()
            stream_copies.append(copy)
        gathers.append(stream_copies)
        forwards[i].append(forward(i, me, 0))

    def pass_on(i):
        for step, copy in enumerate(gathers[i]):
            copy.wait()
            source = lax.rem(chip + chips - 1 - step, chips) * CORES + core
            forwards[i].append(forward(i, source, step + 1))

    def settle(i):
        for copy in forwards[i]:
            copy.wait()

    pass_on(0)
    settle(0)
    if fused:
        query_load.wait()
        head_size = gain_ref.shape[1]
        heads = weights_ref.shape[0]
        group_size = heads // (gathered.shape[3] // head_size)
        scale = math.log2(math.e) / math.sqrt(head_size)

        def weigh(head):
            start = head // group_size * head_size
            keys = gathered[0, :, :, start : start + head_size].reshape(-1, head_size)
            keys = jnp.concatenate([keys, row_mark[...]], axis=1)
            marked = jnp.concatenate([queries[:, head * head_size : (head + 1) * head_size], marks[...]], axis=1)
            scores = lax.dot_general(marked, keys, (((1,), (1,)), ((), ())), preferred_element_type=jnp.float32)
            row_max = jnp.maximum(jnp.max(scores, axis=1, keepdims=True), -1e29)
            weights_ref[head] = jnp.exp2((scores - row_max) * scale).astype(jnp.bfloat16)

        early = min(EARLY_HEADS, heads)
        for head in range(early):
            weigh(head)
        pass_on(1)
        for head in range(early, heads):
            weigh(head)
    else:
        pass_on(1)
        keys_ref[...] = gathered[0]
    settle(1)
    values_ref[...] = gathered[1]


def project(vision, w_key, w_value, key_gain, extra):
    shards = lax.axis_size("seq")
    chips = shards // CORES
    rows, full = vision.shape
    depth, kv_width = w_key.shape
    head_size = key_gain.shape[0]
    fused = bool(extra)
    block = jax.ShapeDtypeStruct((shards, rows, kv_width), jnp.bfloat16)
    dma = pltpu.SemaphoreType.DMA
    hops = chips - 1
    f32, bf16 = jnp.float32, jnp.bfloat16
    hbm, vmem = pl.BlockSpec(memory_space=pltpu.HBM), pl.BlockSpec(memory_space=pltpu.VMEM)
    inputs = (vision, w_key, w_value, key_gain.reshape(1, -1), *extra)
    extra_scratch = []
    first = block
    if fused:
        tokens, query_width = extra[2].shape
        first = jax.ShapeDtypeStruct((query_width // head_size, tokens, shards * rows), bf16)
        extra_scratch = [
            pltpu.SMEM(extra[0].shape, jnp.int32),
            pltpu.VMEM(extra[1].shape, jnp.int32),
            pltpu.VMEM((tokens, query_width), bf16),
            pltpu.VMEM((tokens, head_size), bf16),
            pltpu.VMEM((shards * rows, head_size), bf16),
            dma((3,)),
        ]
    return pl.pallas_call(
        functools.partial(project_kernel, chips, fused),
        out_shape=(first, block),
        in_specs=[hbm] * len(inputs),
        out_specs=(vmem, vmem),
        scratch_shapes=[
            *extra_scratch,
            pltpu.VMEM((1, head_size), f32),
            dma,
            pltpu.VMEM((rows, full), bf16),
            pltpu.VMEM((chips, rows, CORES * depth), bf16),
            pltpu.VMEM((2, CORES * depth, kv_width), bf16),
            pltpu.VMEM((chips, rows, kv_width), f32),
            pltpu.VMEM((2, chips, rows, kv_width), LINK),
            pltpu.VMEM((2, hops, rows, kv_width), LINK),
            pltpu.VMEM((2, shards, rows, kv_width), bf16),
            dma, dma((2,)), dma((2,)), dma((2,)), dma((hops,)), dma((hops,)),
            dma((2, hops)), dma((2, hops)), dma((2, hops)), dma((2, hops)), dma((2, chips)), dma((2, chips)),
        ],
        compiler_params=pltpu.CompilerParams(
            collective_id=0, has_side_effects=True, vmem_limit_bytes=24 * MIB
        ),
        name="project",
    )(*[pltpu.with_memory_space_constraint(each, pltpu.HBM) for each in inputs])


def mix_kernel(head_size, weights_ref, values_ref, out_hbm, mixed, out_sem):
    heads, _, vision_rows = weights_ref.shape
    kv_heads = values_ref.shape[1] // head_size
    group_size = heads // kv_heads
    ones = jnp.ones((vision_rows, head_size), jnp.bfloat16)
    stores = []
    for head in range(heads):
        start = head // group_size * head_size
        values = jnp.concatenate([values_ref[:, start : start + head_size], ones], axis=1)
        summed = jnp.dot(weights_ref[head], values, preferred_element_type=jnp.float32)
        weighted, row_sum = summed[:, :head_size], summed[:, head_size:]
        mixed[:, head * head_size : (head + 1) * head_size] = (
            weighted / jnp.maximum(row_sum, 1.0)
        ).astype(jnp.bfloat16)
        if (head + 1) % STORE_HEADS == 0 or head + 1 == heads:
            first = head // STORE_HEADS * STORE_HEADS
            part = pl.ds(first * head_size, (head + 1 - first) * head_size)
            store = pltpu.make_async_copy(mixed.at[:, part], out_hbm.at[:, part], out_sem.at[len(stores)])
            store.start()
            stores.append(store)
    for store in stores:
        store.wait()


def mix(weights, values, head_size):
    heads, tokens, _ = weights.shape
    vmem = pl.BlockSpec(memory_space=pltpu.VMEM)
    return pl.pallas_call(
        functools.partial(mix_kernel, head_size),
        out_shape=jax.ShapeDtypeStruct((tokens, heads * head_size), jnp.bfloat16),
        in_specs=[vmem, vmem],
        out_specs=pl.BlockSpec(memory_space=pl.ANY),
        scratch_shapes=[
            pltpu.VMEM((tokens, heads * head_size), jnp.bfloat16),
            pltpu.SemaphoreType.DMA((pl.cdiv(heads, STORE_HEADS),)),
        ],
        compiler_params=pltpu.CompilerParams(vmem_limit_bytes=16 * MIB),
        name="mix",
    )(weights, values)


def attend_kernel(head_size, counts_ref, range_ref, queries_ref, keys_ref, values_ref, out_ref, marks, row_mark):
    vision_rows = keys_ref.shape[0]

    @pl.when(pl.program_id(0) == 0)
    def _():
        marks[...] = token_marks(range_ref, counts_ref.shape[0], head_size)
        row_mark[...] = row_marks(counts_ref, vision_rows, head_size)

    scale = math.log2(math.e) / math.sqrt(head_size)
    kv_block = keys_ref.shape[1] // head_size
    group_width = queries_ref.shape[1] // kv_block
    ones = jnp.ones((vision_rows, head_size), jnp.bfloat16)
    for kv_head in range(kv_block):
        kv_part = pl.ds(kv_head * head_size, head_size)
        keys = jnp.concatenate([keys_ref[:, kv_part], row_mark[...]], axis=1)
        values = jnp.concatenate([values_ref[:, kv_part], ones], axis=1)
        for start in range(kv_head * group_width, (kv_head + 1) * group_width, head_size):
            head = pl.ds(start, head_size)
            marked = jnp.concatenate([queries_ref[:, head], marks[...]], axis=1)
            scores = lax.dot_general(marked, keys, (((1,), (1,)), ((), ())), preferred_element_type=jnp.float32)
            row_max = jnp.maximum(jnp.max(scores, axis=1, keepdims=True), -1e29)
            weights = jnp.exp2((scores - row_max) * scale).astype(jnp.bfloat16)
            summed = jnp.dot(weights, values, preferred_element_type=jnp.float32)
            weighted, row_sum = summed[:, :head_size], summed[:, head_size:]
            out_ref[:, head] = (weighted / jnp.maximum(row_sum, 1.0)).astype(jnp.bfloat16)


def attend(queries, keys, values, image_range, image_counts, head_size):
    tokens, query_width = queries.shape
    vision_rows, kv_width = keys.shape
    steps = math.gcd(kv_width // head_size, STEPS)
    group_width = query_width // steps
    kv_block = kv_width // steps
    return pl.pallas_call(
        functools.partial(attend_kernel, head_size),
        out_shape=jax.ShapeDtypeStruct(queries.shape, jnp.bfloat16),
        grid=(steps,),
        in_specs=[
            pl.BlockSpec(memory_space=pltpu.SMEM),
            pl.BlockSpec((2, tokens), lambda h: (0, 0)),
            pl.BlockSpec((tokens, group_width), lambda h: (0, h)),
            pl.BlockSpec((vision_rows, kv_block), lambda h: (0, h)),
            pl.BlockSpec((vision_rows, kv_block), lambda h: (0, h)),
        ],
        out_specs=pl.BlockSpec((tokens, group_width), lambda h: (0, h)),
        scratch_shapes=[
            pltpu.VMEM((tokens, head_size), jnp.bfloat16),
            pltpu.VMEM((vision_rows, head_size), jnp.bfloat16),
        ],
        name="attend",
    )(image_counts, image_range.T, queries, keys, values)


def per_device(queries, vision, w_key, w_value, key_gain, image_range, image_counts):
    head_size = key_gain.shape[0]
    tokens, query_width = queries.shape
    vision_rows = vision.shape[0] * lax.axis_size("seq")
    weight_bytes = query_width // head_size * tokens * vision_rows * 2
    fused = weight_bytes <= WEIGHTS_MAX
    extra = (image_counts, image_range.T, queries) if fused else ()
    first, values = project(vision, w_key, w_value, key_gain, extra)
    values = values.reshape(vision_rows, -1)
    if fused:
        return mix(first, values, head_size)
    return attend(queries, first.reshape(vision_rows, -1), values, image_range, image_counts, head_size)


def solution(mesh):
    placed = (
        P(("groups", "seq"), None),
        P(("groups", "seq"), None),
        P("seq", None),
        P("seq", None),
        P(),
        P(("groups", "seq"), None),
        P("groups"),
    )
    return jax.shard_map(
        per_device,
        mesh=mesh,
        in_specs=placed,
        out_specs=P(("groups", "seq"), None),
        check_vma=False,
    )
```

time: 35.9 us -> 31.4 us (0.87)
  Pallas kernels: 35.7 us -> 31.2 us
    pallas_call x2, Pallas kernels: 35.7 us -> 31.2 us  [the longest x1 29.2 us: project(): pl.pallas_call(functools.partial(project_kernel, chips, fused), out_shape...]
where the time goes in v2:
time: 31.4 us; the launch traced here: 31.2 us
  Pallas kernels  31.2 us (99%)
    pallas_call x1, Pallas kernels, project(): pl.pallas_call(functools.partial(project_kernel, chips, fused), out_shape...  29.2 us
    pallas_call x1, Pallas kernels, mix(): pl.pallas_call(functools.partial(mix_kernel, head_size), out_shape=jax.Sh...  2.04 us

profile of v2, /device:TPU:0, one launch (start us, length us, event | category | flops | bytes accessed | tf_op | source)
XLA Modules:
  0.0 31.2 jit_solution(10695811647883541404)
XLA Ops:
  0.0 29.2 %project.1 = (bf16[32,256,256]{2,1,0:T(8,128)(2,1)S(1)}, bf16[16,16,512]{2,1,0:T(8,128)(2,1)S(1)}) custom-call(bf16[16,8192]{1,0:T(8,128)(2,1)} %refs_0_.1, bf16[512,512]{1,0:T(8,128)(2,1)} %refs_1_.1, bf16[512,512]{1,0:T(8,128)(2,1)} %refs_2_.1, f32[1,128]{1,0:T(1,128)} %bitcast.5, s32[4]{0:T(128)} %refs_4_.1, s32[2,256]{1,0:T(2,128)} %bitcast.4, ...), custom_call_target="tpu_custom_call" | custom-call | tf_op jit(solution)/shard_map/project/pallas_call | solution.py:249
  29.2 2.0 %mix.1 = bf16[256,4096]{1,0:T(8,128)(2,1)} custom-call(bf16[32,256,256]{2,1,0:T(8,128)(2,1)S(1)} %get-tuple-element.7.weights_ref, bf16[256,512]{1,0:T(8,128)(2,1)S(1)} %bitcast.3), custom_call_target="tpu_custom_call" | custom-call | tf_op jit(solution)/shard_map/mix/pallas_call | solution.py:302

commit v3 on v2

--- a/solution.py
+++ b/solution.py
@@ -75,7 +75,9 @@
     width = CORES * depth
     rows = columns.shape[1]
     partner = (group, chip * CORES + (1 - core))
+    hops = chips - 1
     peers = [lax.rem(chip + step, chips) for step in range(1, chips)]
+    sources = [lax.rem(chip + chips - step, chips) for step in range(1, chips)]
 
     def at(chip_index):
         return (group, chip_index * CORES + core)
@@ -116,9 +118,9 @@
 
     load.wait()
     vision_copies = []
-    for step, peer in enumerate(peers):
+    for step, peer in reversed(list(enumerate(peers))):
         part = pl.ds(pl.multiple_of(peer * width, 128), width)
-        copy = remote(vision.at[:, part], columns.at[chip], vision_send.at[step], vision_recv.at[step], at(peer))
+        copy = remote(vision.at[:, part], columns.at[step], vision_send.at[step], vision_recv.at[step], at(peer))
         copy.start()
         vision_copies.append(copy)
     for copy in weight_loads:
@@ -129,7 +131,7 @@
     ]
     for copy in weight_sends:
         copy.start()
-    columns[chip] = vision[:, pl.ds(pl.multiple_of(chip * width, 128), width)]
+    columns[hops] = vision[:, pl.ds(pl.multiple_of(chip * width, 128), width)]
     gain_load.wait()
     if fused:
         counts_load.wait()
@@ -138,23 +140,23 @@
         row_mark[...] = row_marks(counts_ref, *row_mark.shape)
     for copy in weight_sends:
         copy.wait()
+
     for copy in vision_copies:
         copy.wait()
 
-    partial_copies = []
+    partial_copies = ([], [])
     for i in range(2):
         left = columns[...].reshape(chips * rows, width)
         product = jnp.dot(left, w_both[i], preferred_element_type=jnp.float32).reshape(chips, rows, -1)
-        sent[i] = product.astype(sent.dtype)
-        partial[...] = product
-        stream_copies = []
-        for step, peer in enumerate(peers):
+        sent[i] = product[:hops].astype(sent.dtype)
+        partial[i] = product[hops]
+        for step in range(hops):
             copy = remote(
-                sent.at[i, peer], arrived.at[i, step], partial_send.at[i, step], partial_recv.at[i, step], at(peer),
+                sent.at[i, step], arrived.at[i, step], partial_send.at[i, step], partial_recv.at[i, step],
+                at(sources[step]),
             )
             copy.start()
-            stream_copies.append(copy)
-        partial_copies.append((stream_copies, partial[chip]))
+            partial_copies[i].append(copy)
 
     def forward(i, source, slot):
         ref = gathered.at[i, source]
@@ -164,8 +166,8 @@
 
     gathers, forwards = [], ([], [])
     for i in range(2):
-        copies, total = partial_copies[i]
-        for step, copy in enumerate(copies):
+        total = partial[i]
+        for step, copy in enumerate(partial_copies[i]):
             copy.wait()
             total = total + arrived[i, step].astype(jnp.float32)
         done = normed_keys(total, gain_ref[...]) if i == 0 else total.astype(jnp.bfloat16)
@@ -180,9 +182,9 @@
         forwards[i].append(forward(i, me, 0))
 
     def pass_on(i):
-        for step, copy in enumerate(gathers[i]):
-            copy.wait()
-            source = lax.rem(chip + chips - 1 - step, chips) * CORES + core
+        for step in reversed(range(hops)):
+            gathers[i][step].wait()
+            source = sources[step] * CORES + core
             forwards[i].append(forward(i, source, step + 1))
 
     def settle(i):
@@ -258,8 +260,8 @@
             pltpu.VMEM((rows, full), bf16),
             pltpu.VMEM((chips, rows, CORES * depth), bf16),
             pltpu.VMEM((2, CORES * depth, kv_width), bf16),
-            pltpu.VMEM((chips, rows, kv_width), f32),
-            pltpu.VMEM((2, chips, rows, kv_width), LINK),
+            pltpu.VMEM((2, rows, kv_width), f32),
+            pltpu.VMEM((2, hops, rows, kv_width), LINK),
             pltpu.VMEM((2, hops, rows, kv_width), LINK),
             pltpu.VMEM((2, shards, rows, kv_width), bf16),
             dma, dma((2,)), dma((2,)), dma((2,)), dma((hops,)), dma((hops,)),

time: 31.4 us -> 28.7 us (0.914)
  Pallas kernels: 31.2 us -> 28.6 us
    pallas_call x1, Pallas kernels: 29.2 us -> 26.5 us  [project(): pl.pallas_call(functools.partial(project_kernel, chips, fused), out_shape...]
where the time goes in v3:
time: 28.7 us; the launch traced here: 28.6 us
  Pallas kernels  28.6 us (100%)
    pallas_call x1, Pallas kernels, project(): pl.pallas_call(functools.partial(project_kernel, chips, fused), out_shape...  26.5 us
    pallas_call x1, Pallas kernels, mix(): pl.pallas_call(functools.partial(mix_kernel, head_size), out_shape=jax.Sh...  2.04 us

profile of v3, /device:TPU:0, one launch (start us, length us, event | category | flops | bytes accessed | tf_op | source)
XLA Modules:
  0.0 28.6 jit_solution(9466073639090825265)
XLA Ops:
  0.0 26.5 %project.1 = (bf16[32,256,256]{2,1,0:T(8,128)(2,1)S(1)}, bf16[16,16,512]{2,1,0:T(8,128)(2,1)S(1)}) custom-call(bf16[16,8192]{1,0:T(8,128)(2,1)} %refs_0_.1, bf16[512,512]{1,0:T(8,128)(2,1)} %refs_1_.1, bf16[512,512]{1,0:T(8,128)(2,1)} %refs_2_.1, f32[1,128]{1,0:T(1,128)} %bitcast.5, s32[4]{0:T(128)} %refs_4_.1, s32[2,256]{1,0:T(2,128)} %bitcast.4, ...), custom_call_target="tpu_custom_call" | custom-call | tf_op jit(solution)/shard_map/project/pallas_call | solution.py:251
  26.5 2.0 %mix.1 = bf16[256,4096]{1,0:T(8,128)(2,1)} custom-call(bf16[32,256,256]{2,1,0:T(8,128)(2,1)S(1)} %get-tuple-element.7.weights_ref, bf16[256,512]{1,0:T(8,128)(2,1)S(1)} %bitcast.3), custom_call_target="tpu_custom_call" | custom-call | tf_op jit(solution)/shard_map/mix/pallas_call | solution.py:304

commit v4 on v3

--- a/solution.py
+++ b/solution.py
@@ -12,7 +12,8 @@
 CORES = 2
 STEPS = 2
 STORE_HEADS = 4
-EARLY_HEADS = 24
+ONES = 16
+EARLY_HEADS = 18
 LINK = jnp.bfloat16
 MASKED = -1e30
 MIB = 1024 * 1024
@@ -205,8 +206,8 @@
             keys = gathered[0, :, :, start : start + head_size].reshape(-1, head_size)
             keys = jnp.concatenate([keys, row_mark[...]], axis=1)
             marked = jnp.concatenate([queries[:, head * head_size : (head + 1) * head_size], marks[...]], axis=1)
-            scores = lax.dot_general(marked, keys, (((1,), (1,)), ((), ())), preferred_element_type=jnp.float32)
-            row_max = jnp.maximum(jnp.max(scores, axis=1, keepdims=True), -1e29)
+            scores = lax.dot_general(keys, marked, (((1,), (1,)), ((), ())), preferred_element_type=jnp.float32)
+            row_max = jnp.maximum(jnp.max(scores, axis=0, keepdims=True), -1e29)
             weights_ref[head] = jnp.exp2((scores - row_max) * scale).astype(jnp.bfloat16)
 
         early = min(EARLY_HEADS, heads)
@@ -239,7 +240,7 @@
     first = block
     if fused:
         tokens, query_width = extra[2].shape
-        first = jax.ShapeDtypeStruct((query_width // head_size, tokens, shards * rows), bf16)
+        first = jax.ShapeDtypeStruct((query_width // head_size, shards * rows, tokens), bf16)
         extra_scratch = [
             pltpu.SMEM(extra[0].shape, jnp.int32),
             pltpu.VMEM(extra[1].shape, jnp.int32),
@@ -275,19 +276,20 @@
 
 
 def mix_kernel(head_size, weights_ref, values_ref, out_hbm, mixed, out_sem):
-    heads, _, vision_rows = weights_ref.shape
+    heads, vision_rows, _ = weights_ref.shape
     kv_heads = values_ref.shape[1] // head_size
     group_size = heads // kv_heads
-    ones = jnp.ones((vision_rows, head_size), jnp.bfloat16)
+    ones = jnp.ones((ONES, vision_rows), jnp.bfloat16)
     stores = []
     for head in range(heads):
-        start = head // group_size * head_size
-        values = jnp.concatenate([values_ref[:, start : start + head_size], ones], axis=1)
-        summed = jnp.dot(weights_ref[head], values, preferred_element_type=jnp.float32)
-        weighted, row_sum = summed[:, :head_size], summed[:, head_size:]
+        if head % group_size == 0:
+            start = head // group_size * head_size
+            values = jnp.concatenate([values_ref[:, start : start + head_size].T, ones], axis=0)
+        summed = jnp.dot(values, weights_ref[head], preferred_element_type=jnp.float32)
+        weighted, row_sum = summed[:head_size], summed[head_size : head_size + 1]
         mixed[:, head * head_size : (head + 1) * head_size] = (
-            weighted / jnp.maximum(row_sum, 1.0)
-        ).astype(jnp.bfloat16)
+            (weighted * (1.0 / jnp.maximum(row_sum, 1.0))).astype(jnp.bfloat16).T
+        )
         if (head + 1) % STORE_HEADS == 0 or head + 1 == heads:
             first = head // STORE_HEADS * STORE_HEADS
             part = pl.ds(first * head_size, (head + 1 - first) * head_size)
@@ -299,7 +301,7 @@
 
 
 def mix(weights, values, head_size):
-    heads, tokens, _ = weights.shape
+    heads, _, tokens = weights.shape
     vmem = pl.BlockSpec(memory_space=pltpu.VMEM)
     return pl.pallas_call(
         functools.partial(mix_kernel, head_size),

time: 28.7 us -> 28.7 us (level)
  no operation moved by 1% of the time
where the time goes in v4:
time: 28.7 us; the launch traced here: 28.5 us
  Pallas kernels  28.5 us (99%)
    pallas_call x1, Pallas kernels, project(): pl.pallas_call(functools.partial(project_kernel, chips, fused), out_shape...  26.7 us
    pallas_call x1, Pallas kernels, mix(): pl.pallas_call(functools.partial(mix_kernel, head_size), out_shape=jax.Sh...  1.85 us

profile of v4, /device:TPU:0, one launch (start us, length us, event | category | flops | bytes accessed | tf_op | source)
XLA Modules:
  0.0 28.5 jit_solution(9161111133556887254)
XLA Ops:
  0.0 26.7 %project.1 = (bf16[32,256,256]{2,1,0:T(8,128)(2,1)S(1)}, bf16[16,16,512]{2,1,0:T(8,128)(2,1)S(1)}) custom-call(bf16[16,8192]{1,0:T(8,128)(2,1)} %refs_0_.1, bf16[512,512]{1,0:T(8,128)(2,1)} %refs_1_.1, bf16[512,512]{1,0:T(8,128)(2,1)} %refs_2_.1, f32[1,128]{1,0:T(1,128)} %bitcast.5, s32[4]{0:T(128)} %refs_4_.1, s32[2,256]{1,0:T(2,128)} %bitcast.4, ...), custom_call_target="tpu_custom_call" | custom-call | tf_op jit(solution)/shard_map/project/pallas_call | solution.py:252
  26.7 1.8 %mix.1 = bf16[256,4096]{1,0:T(8,128)(2,1)} custom-call(bf16[32,256,256]{2,1,0:T(8,128)(2,1)S(1)} %get-tuple-element.7.weights_ref, bf16[256,512]{1,0:T(8,128)(2,1)S(1)} %bitcast.3), custom_call_target="tpu_custom_call" | custom-call | tf_op jit(solution)/shard_map/mix/pallas_call | solution.py:306

commit v5 on v3

--- a/solution.py
+++ b/solution.py
@@ -12,7 +12,7 @@
 CORES = 2
 STEPS = 2
 STORE_HEADS = 4
-EARLY_HEADS = 24
+EARLY_HEADS = 18
 LINK = jnp.bfloat16
 MASKED = -1e30
 MIB = 1024 * 1024

time: 28.7 us -> 28.6 us (level)
  no operation moved by 1% of the time
where the time goes in v5:
time: 28.6 us; the launch traced here: 28.4 us
  Pallas kernels  28.4 us (99%)
    pallas_call x1, Pallas kernels, project(): pl.pallas_call(functools.partial(project_kernel, chips, fused), out_shape...  26.4 us
    pallas_call x1, Pallas kernels, mix(): pl.pallas_call(functools.partial(mix_kernel, head_size), out_shape=jax.Sh...  2.04 us

profile of v5, /device:TPU:0, one launch (start us, length us, event | category | flops | bytes accessed | tf_op | source)
XLA Modules:
  0.0 28.4 jit_solution(12687394496117505027)
XLA Ops:
  0.0 26.4 %project.1 = (bf16[32,256,256]{2,1,0:T(8,128)(2,1)S(1)}, bf16[16,16,512]{2,1,0:T(8,128)(2,1)S(1)}) custom-call(bf16[16,8192]{1,0:T(8,128)(2,1)} %refs_0_.1, bf16[512,512]{1,0:T(8,128)(2,1)} %refs_1_.1, bf16[512,512]{1,0:T(8,128)(2,1)} %refs_2_.1, f32[1,128]{1,0:T(1,128)} %bitcast.5, s32[4]{0:T(128)} %refs_4_.1, s32[2,256]{1,0:T(2,128)} %bitcast.4, ...), custom_call_target="tpu_custom_call" | custom-call | tf_op jit(solution)/shard_map/project/pallas_call | solution.py:251
  26.4 2.0 %mix.1 = bf16[256,4096]{1,0:T(8,128)(2,1)} custom-call(bf16[32,256,256]{2,1,0:T(8,128)(2,1)S(1)} %get-tuple-element.7.weights_ref, bf16[256,512]{1,0:T(8,128)(2,1)S(1)} %bitcast.3), custom_call_target="tpu_custom_call" | custom-call | tf_op jit(solution)/shard_map/mix/pallas_call | solution.py:304
